TPU v7x, 32 devices: a whole 2x2x4 slice. The times are simulated.
32 devices in a mesh: rows: 4 (over z), feat: 8 (over y, x, core).
Axes of the slice: x: 2, y: 2, z: 4, core: 2. Of those that a mesh axis runs over, the one named last changes fastest.
Arguments:
- codes: int32 [65536, 512], P(('rows', 'feat')), may hold values from 0 to 255, as said below
- node_ids: int32 [2, 65536], P(None, ('rows', 'feat')), may hold values from 0 to 3
- bag_counts: int32 [2, 65536], P(None, ('rows', 'feat')), may hold values from 0 to 3
- labels: int32 [65536], P(('rows', 'feat')), may hold values from 0 to 1
Outputs:
- feature_gain: float32 [2, 4, 512], P(None, None, 'feat')
- node_gain: float32 [2, 4], replicated
Inputs may be any that keep to these rules, and one draw needn't show every extreme that they name: Each feature's codes lie below a cap of that feature; bins above the cap are empty.
All inputs are finite; a program needn't handle non-finite values.
Results may differ from a plain program's by a relative error of at most 0.0003.
Values sent between devices are 32-bit elements; how exact they have to be, the bound alone decides.
A program may use at most 64 MiB of HBM per device.

v0:
```python
import math

import jax
import jax.numpy as jnp
from jax import lax
from jax.sharding import PartitionSpec as P

BINS = 256
CLASSES = 2
TREES = 2
NODES = 4


def make_weights(node_ids, bag_counts, labels):
    trees, count_rows = node_ids.shape
    node_range = jnp.arange(NODES, dtype=jnp.int32)
    class_range = jnp.arange(CLASSES, dtype=jnp.int32)
    node_hit = (node_ids[:, :, None] == node_range).astype(jnp.float32)
    class_hit = (labels[:, None] == class_range).astype(jnp.float32)
    weights = (
        bag_counts.astype(jnp.float32)[:, :, None, None]
        * node_hit[:, :, :, None]
        * class_hit[None, :, None, :]
    )
    return (
        jnp.transpose(weights, (1, 0, 2, 3))
        .reshape(count_rows, trees * NODES * CLASSES)
        .astype(jnp.bfloat16)
    )


def split_gains(left):
    feats = left.shape[0]
    left = left.reshape(feats, TREES, NODES, CLASSES, left.shape[-1])
    total = left[..., -1:]
    n_left = jnp.sum(left, axis=3, keepdims=True)
    n_total = jnp.sum(total, axis=3, keepdims=True)
    n_right = n_total - n_left
    frac = n_left / jnp.maximum(n_total, 1.0)
    spread_terms = (left - total * frac) ** 2
    scaled = n_total / (jnp.maximum(n_left, 1.0) * jnp.maximum(n_right, 1.0))
    spread = jnp.sum(spread_terms * scaled, axis=3)
    best = jnp.max(spread, axis=-1)
    return jnp.transpose(best, (1, 2, 0))


def gains_of(hist):
    bin_index = jnp.arange(BINS, dtype=jnp.int32)
    upper = (bin_index[:, None] <= bin_index[None, :]).astype(jnp.float32)
    left = jnp.einsum("fsb,bk->fsk", hist, upper, precision=lax.Precision.HIGHEST)
    return split_gains(left)


def histogram_of(columns, weights):
    count_rows, count = columns.shape
    block_size = math.gcd(count, 32)
    blocks = jnp.transpose(columns.reshape(count_rows, count // block_size, block_size), (1, 0, 2))
    bin_index = jnp.arange(BINS, dtype=jnp.int32)

    def one_block(column_block):
        onehot = (column_block[:, :, None] == bin_index).astype(jnp.bfloat16)
        return jnp.einsum("rfb,rs->fsb", onehot, weights, preferred_element_type=jnp.float32)

    summed = lax.map(one_block, blocks)
    return summed.reshape(count, weights.shape[1], BINS)


def on_device(codes, node_ids, bag_counts, labels):
    weights = make_weights(node_ids, bag_counts, labels)
    partial_hist = lax.psum_scatter(
        histogram_of(codes, weights), "feat", scatter_dimension=0, tiled=True
    )
    hist = lax.psum(partial_hist, "rows")
    feature_gain = gains_of(hist)
    node_gain = lax.pmax(jnp.max(feature_gain, axis=2), "feat")
    return (feature_gain, node_gain)


def solution(mesh):
    return jax.shard_map(
        on_device,
        mesh=mesh,
        in_specs=(
            P(("rows", "feat"), None),
            P(None, ("rows", "feat")),
            P(None, ("rows", "feat")),
            P(("rows", "feat")),
        ),
        out_specs=(P(None, None, "feat"), P()),
        check_vma=False,
    )
```

profile of v0, /device:TPU:0, one launch (start us, length us, event | category | flops | bytes accessed | tf_op | source)
XLA Modules:
  0.0 460.7 jit_solution(4944158148707824612)
XLA Ops:
  7.2 5.4 %copy.20 = s32[2048,512]{0,1:T(8,128)} copy(s32[2048,512]{1,0:T(8,128)} %param.6) | data formatting | bytes 8388608 | tf_op args[0]
  12.8 286.6 %while.11 = (s32[]{:T(128)}, f32[16,32,16,256]{3,2,1,0:T(8,128)}, s32[16,2048,32]{1,2,0:T(8,128)}, f32[2048,2]{0,1:T(2,128)S(1)}, f32[2048,2,4]{0,2,1:T(4,128)S(1)}, /*index=5*/s32[]{:T(128)}) while((s32[]{:T(128)}, f32[16,32,16,256]{3,2,1,0:T(8,128)}, s32[16,2048,32]{1,2,0:T(8,128)}, f32[2048,2]{0,1:T(2,128)S(1)}, ...), condition=%wide.region_1.2_spmd.clone, body=%wide.region_0.1_spmd.clone.sunk | while | flops 553713664 | bytes 1655369 | solution.py:64
  12.8 1.0 dynamic-slice_bitcast_fusion.2
  13.9 16.8 %fusion.19 = f32[16,32,16,256]{3,2,1,0:T(8,128)} fusion(f32[16,32,16,256]{3,2,1,0:T(8,128)} %get-tuple-element.97, s32[]{:T(128)} %get-tuple-element.96, bf16[2048,16,1]{0,1,2:T(8,128)(2,1)S(1)} %reshape.85, s32[2048,32]{0,1:T(8,128)S(1)} %dynamic-slice_bitcast_fusion.2), kind=kOutput, calls=%fused_computation.6.clone.2 | convolution fusion | flops 553648128 | bytes 852480 | tf_op jit(solution)/shard_map/while/body/eval_jaxpr/rfb,rs->fsb/dot_general | solution.py:62
  30.7 1.0 dynamic-slice_bitcast_fusion.2
  31.8 16.8 %fusion.19 = f32[16,32,16,256]{3,2,1,0:T(8,128)} fusion(f32[16,32,16,256]{3,2,1,0:T(8,128)} %get-tuple-element.97, s32[]{:T(128)} %get-tuple-element.96, bf16[2048,16,1]{0,1,2:T(8,128)(2,1)S(1)} %reshape.85, s32[2048,32]{0,1:T(8,128)S(1)} %dynamic-slice_bitcast_fusion.2), kind=kOutput, calls=%fused_computation.6.clone.2 | convolution fusion | flops 553648128 | bytes 852480 | tf_op jit(solution)/shard_map/while/body/eval_jaxpr/rfb,rs->fsb/dot_general | solution.py:62
  49.7 16.8 %fusion.19 = f32[16,32,16,256]{3,2,1,0:T(8,128)} fusion(f32[16,32,16,256]{3,2,1,0:T(8,128)} %get-tuple-element.97, s32[]{:T(128)} %get-tuple-element.96, bf16[2048,16,1]{0,1,2:T(8,128)(2,1)S(1)} %reshape.85, s32[2048,32]{0,1:T(8,128)S(1)} %dynamic-slice_bitcast_fusion.2), kind=kOutput, calls=%fused_computation.6.clone.2 | convolution fusion | flops 553648128 | bytes 852480 | tf_op jit(solution)/shard_map/while/body/eval_jaxpr/rfb,rs->fsb/dot_general | solution.py:62
  67.6 16.8 %fusion.19 = f32[16,32,16,256]{3,2,1,0:T(8,128)} fusion(f32[16,32,16,256]{3,2,1,0:T(8,128)} %get-tuple-element.97, s32[]{:T(128)} %get-tuple-element.96, bf16[2048,16,1]{0,1,2:T(8,128)(2,1)S(1)} %reshape.85, s32[2048,32]{0,1:T(8,128)S(1)} %dynamic-slice_bitcast_fusion.2), kind=kOutput, calls=%fused_computation.6.clone.2 | convolution fusion | flops 553648128 | bytes 852480 | tf_op jit(solution)/shard_map/while/body/eval_jaxpr/rfb,rs->fsb/dot_general | solution.py:62
  85.5 16.8 %fusion.19 = f32[16,32,16,256]{3,2,1,0:T(8,128)} fusion(f32[16,32,16,256]{3,2,1,0:T(8,128)} %get-tuple-element.97, s32[]{:T(128)} %get-tuple-element.96, bf16[2048,16,1]{0,1,2:T(8,128)(2,1)S(1)} %reshape.85, s32[2048,32]{0,1:T(8,128)S(1)} %dynamic-slice_bitcast_fusion.2), kind=kOutput, calls=%fused_computation.6.clone.2 | convolution fusion | flops 553648128 | bytes 852480 | tf_op jit(solution)/shard_map/while/body/eval_jaxpr/rfb,rs->fsb/dot_general | solution.py:62
  103.4 16.8 %fusion.19 = f32[16,32,16,256]{3,2,1,0:T(8,128)} fusion(f32[16,32,16,256]{3,2,1,0:T(8,128)} %get-tuple-element.97, s32[]{:T(128)} %get-tuple-element.96, bf16[2048,16,1]{0,1,2:T(8,128)(2,1)S(1)} %reshape.85, s32[2048,32]{0,1:T(8,128)S(1)} %dynamic-slice_bitcast_fusion.2), kind=kOutput, calls=%fused_computation.6.clone.2 | convolution fusion | flops 553648128 | bytes 852480 | tf_op jit(solution)/shard_map/while/body/eval_jaxpr/rfb,rs->fsb/dot_general | solution.py:62
  120.2 1.0 dynamic-slice_bitcast_fusion.2
  121.3 16.8 %fusion.19 = f32[16,32,16,256]{3,2,1,0:T(8,128)} fusion(f32[16,32,16,256]{3,2,1,0:T(8,128)} %get-tuple-element.97, s32[]{:T(128)} %get-tuple-element.96, bf16[2048,16,1]{0,1,2:T(8,128)(2,1)S(1)} %reshape.85, s32[2048,32]{0,1:T(8,128)S(1)} %dynamic-slice_bitcast_fusion.2), kind=kOutput, calls=%fused_computation.6.clone.2 | convolution fusion | flops 553648128 | bytes 852480 | tf_op jit(solution)/shard_map/while/body/eval_jaxpr/rfb,rs->fsb/dot_general | solution.py:62
  138.1 1.0 dynamic-slice_bitcast_fusion.2
  139.2 16.8 %fusion.19 = f32[16,32,16,256]{3,2,1,0:T(8,128)} fusion(f32[16,32,16,256]{3,2,1,0:T(8,128)} %get-tuple-element.97, s32[]{:T(128)} %get-tuple-element.96, bf16[2048,16,1]{0,1,2:T(8,128)(2,1)S(1)} %reshape.85, s32[2048,32]{0,1:T(8,128)S(1)} %dynamic-slice_bitcast_fusion.2), kind=kOutput, calls=%fused_computation.6.clone.2 | convolution fusion | flops 553648128 | bytes 852480 | tf_op jit(solution)/shard_map/while/body/eval_jaxpr/rfb,rs->fsb/dot_general | solution.py:62
  156.1 1.0 dynamic-slice_bitcast_fusion.2
  157.1 16.8 %fusion.19 = f32[16,32,16,256]{3,2,1,0:T(8,128)} fusion(f32[16,32,16,256]{3,2,1,0:T(8,128)} %get-tuple-element.97, s32[]{:T(128)} %get-tuple-element.96, bf16[2048,16,1]{0,1,2:T(8,128)(2,1)S(1)} %reshape.85, s32[2048,32]{0,1:T(8,128)S(1)} %dynamic-slice_bitcast_fusion.2), kind=kOutput, calls=%fused_computation.6.clone.2 | convolution fusion | flops 553648128 | bytes 852480 | tf_op jit(solution)/shard_map/while/body/eval_jaxpr/rfb,rs->fsb/dot_general | solution.py:62
  174.0 1.0 dynamic-slice_bitcast_fusion.2
  175.0 16.8 %fusion.19 = f32[16,32,16,256]{3,2,1,0:T(8,128)} fusion(f32[16,32,16,256]{3,2,1,0:T(8,128)} %get-tuple-element.97, s32[]{:T(128)} %get-tuple-element.96, bf16[2048,16,1]{0,1,2:T(8,128)(2,1)S(1)} %reshape.85, s32[2048,32]{0,1:T(8,128)S(1)} %dynamic-slice_bitcast_fusion.2), kind=kOutput, calls=%fused_computation.6.clone.2 | convolution fusion | flops 553648128 | bytes 852480 | tf_op jit(solution)/shard_map/while/body/eval_jaxpr/rfb,rs->fsb/dot_general | solution.py:62
  192.9 16.8 %fusion.19 = f32[16,32,16,256]{3,2,1,0:T(8,128)} fusion(f32[16,32,16,256]{3,2,1,0:T(8,128)} %get-tuple-element.97, s32[]{:T(128)} %get-tuple-element.96, bf16[2048,16,1]{0,1,2:T(8,128)(2,1)S(1)} %reshape.85, s32[2048,32]{0,1:T(8,128)S(1)} %dynamic-slice_bitcast_fusion.2), kind=kOutput, calls=%fused_computation.6.clone.2 | convolution fusion | flops 553648128 | bytes 852480 | tf_op jit(solution)/shard_map/while/body/eval_jaxpr/rfb,rs->fsb/dot_general | solution.py:62
  210.8 16.8 %fusion.19 = f32[16,32,16,256]{3,2,1,0:T(8,128)} fusion(f32[16,32,16,256]{3,2,1,0:T(8,128)} %get-tuple-element.97, s32[]{:T(128)} %get-tuple-element.96, bf16[2048,16,1]{0,1,2:T(8,128)(2,1)S(1)} %reshape.85, s32[2048,32]{0,1:T(8,128)S(1)} %dynamic-slice_bitcast_fusion.2), kind=kOutput, calls=%fused_computation.6.clone.2 | convolution fusion | flops 553648128 | bytes 852480 | tf_op jit(solution)/shard_map/while/body/eval_jaxpr/rfb,rs->fsb/dot_general | solution.py:62
  228.8 16.8 %fusion.19 = f32[16,32,16,256]{3,2,1,0:T(8,128)} fusion(f32[16,32,16,256]{3,2,1,0:T(8,128)} %get-tuple-element.97, s32[]{:T(128)} %get-tuple-element.96, bf16[2048,16,1]{0,1,2:T(8,128)(2,1)S(1)} %reshape.85, s32[2048,32]{0,1:T(8,128)S(1)} %dynamic-slice_bitcast_fusion.2), kind=kOutput, calls=%fused_computation.6.clone.2 | convolution fusion | flops 553648128 | bytes 852480 | tf_op jit(solution)/shard_map/while/body/eval_jaxpr/rfb,rs->fsb/dot_general | solution.py:62
  246.7 16.8 %fusion.19 = f32[16,32,16,256]{3,2,1,0:T(8,128)} fusion(f32[16,32,16,256]{3,2,1,0:T(8,128)} %get-tuple-element.97, s32[]{:T(128)} %get-tuple-element.96, bf16[2048,16,1]{0,1,2:T(8,128)(2,1)S(1)} %reshape.85, s32[2048,32]{0,1:T(8,128)S(1)} %dynamic-slice_bitcast_fusion.2), kind=kOutput, calls=%fused_computation.6.clone.2 | convolution fusion | flops 553648128 | bytes 852480 | tf_op jit(solution)/shard_map/while/body/eval_jaxpr/rfb,rs->fsb/dot_general | solution.py:62
  264.6 16.8 %fusion.19 = f32[16,32,16,256]{3,2,1,0:T(8,128)} fusion(f32[16,32,16,256]{3,2,1,0:T(8,128)} %get-tuple-element.97, s32[]{:T(128)} %get-tuple-element.96, bf16[2048,16,1]{0,1,2:T(8,128)(2,1)S(1)} %reshape.85, s32[2048,32]{0,1:T(8,128)S(1)} %dynamic-slice_bitcast_fusion.2), kind=kOutput, calls=%fused_computation.6.clone.2 | convolution fusion | flops 553648128 | bytes 852480 | tf_op jit(solution)/shard_map/while/body/eval_jaxpr/rfb,rs->fsb/dot_general | solution.py:62
  282.5 16.8 %fusion.19 = f32[16,32,16,256]{3,2,1,0:T(8,128)} fusion(f32[16,32,16,256]{3,2,1,0:T(8,128)} %get-tuple-element.97, s32[]{:T(128)} %get-tuple-element.96, bf16[2048,16,1]{0,1,2:T(8,128)(2,1)S(1)} %reshape.85, s32[2048,32]{0,1:T(8,128)S(1)} %dynamic-slice_bitcast_fusion.2), kind=kOutput, calls=%fused_computation.6.clone.2 | convolution fusion | flops 553648128 | bytes 852480 | tf_op jit(solution)/shard_map/while/body/eval_jaxpr/rfb,rs->fsb/dot_general | solution.py:62
  299.4 74.3 %reduce-scatter.2.cloned.1.call-done = f32[64,16,256]{2,1,0:T(8,128)} async-done(((f32[512,16,256]{2,1,0:T(8,128)}), f32[64,16,256]{2,1,0:T(8,128)}) %reduce-scatter.2.cloned.1.call-update) | async-done | bytes 1048592 | tf_op jit(solution)/shard_map/reduce_scatter | solution.py:70
  373.8 54.3 %all-reduce.2.cloned.1.call-done = f32[64,16,256]{2,1,0:T(8,128)} async-done(((f32[64,16,256]{2,1,0:T(8,128)}), f32[64,16,256]{2,1,0:T(8,128)}) %all-reduce.2.cloned.1.call-update) | async-done | bytes 1048592 | tf_op jit(solution)/shard_map/psum | solution.py:73
  428.0 1.8 fusion.9
  430.5 1.4 fusion.12
  432.1 1.5 reduce_sum.27
  433.6 3.1 copy.28
  437.1 2.0 multiply_reduce_fusion
  439.6 14.3 %pmax.7 = f32[2,4]{1,0:T(2,128)} all-reduce(f32[2,4]{1,0:T(2,128)S(1)} %bitcast_reduce_fusion), channel_id=1, replica_groups=mesh['rows'=4,'feat'=8] {'feat'}, use_global_device_ids=true, to_apply=%region_9.10 | all-reduce | flops 8 | bytes 64 | tf_op jit(solution)/shard_map/pmax | solution.py:75
  (66 shorter events, 12.8 us)
Async XLA Ops:
  7.2 5.5 %copy-start.1 = (s32[2,2048]{1,0:T(2,128)S(1)}, s32[2,2048]{1,0:T(2,128)}, u32[]{:S(2)}) copy-start(s32[2,2048]{1,0:T(2,128)} %param.8) | copy-start | bytes 49156
  7.2 5.5 %copy-start.3 = (s32[2048]{0:T(1024)S(1)}, s32[2048]{0:T(1024)}, u32[]{:S(2)}) copy-start(s32[2048]{0:T(1024)} %param.9) | copy-start | bytes 24580
  7.2 5.5 %copy-start.2 = (s32[2,2048]{1,0:T(2,128)S(1)}, s32[2,2048]{1,0:T(2,128)}, u32[]{:S(2)}) copy-start(s32[2,2048]{1,0:T(2,128)} %param.7) | copy-start | bytes 49156
  7.2 366.5 %reduce-scatter.2.cloned.1.call-start = ((), (), s32[]{:S(2)}) async-start(), calls=%async_computation.1 | async-start | bytes 9437184 | tf_op jit(solution)/shard_map/reduce_scatter | solution.py:70
  299.4 128.7 %all-reduce.2.cloned.1.call-start = ((), (), s32[]{:S(2)}) async-start(), calls=%async_computation.2 | async-start | bytes 2097152 | tf_op jit(solution)/shard_map/psum | solution.py:73
  439.5 14.3 %copy-start = (f32[64,2,4]{0,2,1:T(4,128)}, f32[64,2,4]{0,2,1:T(4,128)S(1)}, u32[]{:S(2)}) copy-start(f32[64,2,4]{0,2,1:T(4,128)S(1)} %copy.26) | copy-start | bytes 6148
Sparse Core Ops, SparseCore 0:
  299.5 74.2 reduce-scatter.1
  376.1 51.8 all-reduce.1
where the time goes:
time: 461 us
  matrix products  271 us (59%)
  waiting for transfers between devices  129 us (28%)
  local copies, waits for them, and re-layouts  25.5 us (6%)
  blocking collectives  14.3 us (3%)
  between operations  14.2 us (3%)
  other arithmetic  6.47 us (1%)
    dot_general x16, matrix products, one_block(): jnp.einsum('rfb,rs->fsb', onehot, weights, preferred_element_type=jnp.flo...  269 us
    reduce_scatter x1, waiting for transfers between devices, on_device(): lax.psum_scatter(histogram_of(codes, weights), 'feat', scatter_dimension=...  74.3 us
    psum x1, waiting for transfers between devices, on_device(): hist = lax.psum(partial_hist, 'rows')  54.3 us
    eq x16, local copies, waits for them, and re-layouts, one_block(): onehot = (column_block[:, :, None] == bin_index).astype(jnp.bfloat16)  15.5 us
    pmax x1, blocking collectives, on_device(): node_gain = lax.pmax(jnp.max(feature_gain, axis=2), 'feat')  14.3 us
  transfers between devices with their start and end apart: 2, of which 2 were waited for; matrix products, arithmetic and copies ran while one was open for 0% of the time, Pallas kernels for 0%

commit v1 on v0

v1 whole, which is shorter than its diff:
```python
import functools
import math

import jax
import jax.numpy as jnp
from jax import lax
from jax.experimental import pallas as pl
from jax.experimental.pallas import tpu as pltpu
from jax.sharding import PartitionSpec as P

BINS = 256
CLASSES = 2
TREES = 2
NODES = 4
TN = TREES * NODES
LOW = 64
HIGH = BINS // LOW
PACK = 4096.0
CHUNK = 1024
GROUP = 4
MESH = pl.DeviceIdType.MESH


def plan(rows, feat, features):
    chips = feat // 2
    xs = 1 << (int(math.log2(chips)) // 2)
    ys = chips // xs
    local = features // feat
    rounds = 2 if local % (2 * 2 * GROUP) == 0 and local % (2 * 2 * rows) == 0 else 1
    return chips, xs, ys, local, rounds


def kernel(rows, feat, features, count_rows, ct_ref, meta_ref, fg_ref, node_ref,
           ct_in, meta_in, hi_ref, lo_ref, w_ref, sbuf, rbuf, zbuf, zup, zdown, gbuf, mbuf, min_ref,
           core_s, core_r, xy_s, xy_r, up_s, up_r, down_s, down_r, g_s, g_r, m_s, m_r):
    chips, xs, ys, local, rounds = plan(rows, feat, features)
    half = local // rounds // 2
    pairs = half // 2
    zb = half * 2 // rows // 2
    me = lax.axis_index("feat")
    z = lax.axis_index("rows")
    core = lax.rem(me, 2)
    chip = lax.div(me, 2)
    x = lax.rem(chip, xs)
    y = lax.div(chip, xs)

    def dev(yy, xx):
        return {"feat": (yy * xs + xx) * 2 + core}

    def feat_peer(k):
        return {"feat": lax.rem(me + k, feat)}

    def row_peer(k):
        return {"rows": lax.rem(z + k, rows)}

    barrier = pltpu.get_barrier_semaphore()
    for k in range(1, feat):
        pl.semaphore_signal(barrier, inc=1, device_id=feat_peer(k), device_id_type=MESH)
    for k in range(1, rows):
        pl.semaphore_signal(barrier, inc=1, device_id=row_peer(k), device_id_type=MESH)
    pl.semaphore_wait(barrier, feat - 1 + rows - 1)

    partner = {"feat": chip * 2 + 1 - core}
    pending = []

    def send(src, dst, s, r, device):
        copy = pltpu.make_async_remote_copy(
            src_ref=src, dst_ref=dst, send_sem=s, recv_sem=r, device_id=device, device_id_type=MESH)
        copy.start()
        pending.append(copy)
        return copy

    swaps = [send(meta_ref, meta_in, core_s.at[chips], core_r.at[chips], partner)]
    for q in range(chips):
        start = pl.multiple_of((2 * q + 1 - core) * local, local)
        swaps.append(send(ct_ref.at[pl.ds(start, local)], ct_in.at[pl.ds(q * local, local)],
                          core_s.at[q], core_r.at[q], partner))

    def weights(meta, base):
        row = lax.broadcasted_iota(jnp.int32, (TN, CHUNK), 0)
        tree = lax.div(row, NODES)
        node = lax.rem(row, NODES).astype(jnp.float32)

        def body(i, _):
            at = pl.ds(pl.multiple_of(i * CHUNK, CHUNK), CHUNK)
            m = meta[:, at]
            ids = jnp.where(tree == 0, m[0:1], m[1:2])
            bags = jnp.where(tree == 0, m[2:3], m[3:4])
            w = jnp.where(ids == node, bags * (1.0 + (PACK - 1.0) * m[4:5]), 0.0)
            out = pl.ds(pl.multiple_of(base + i * CHUNK, CHUNK), CHUNK)
            w_ref[:, out] = jnp.concatenate([w] * HIGH, axis=0).astype(jnp.bfloat16)
            return 0

        lax.fori_loop(0, count_rows // CHUNK, body, 0)

    def split(src, start, q, base):
        def body(i, _):
            code = src[pl.ds(pl.multiple_of(start + i * 8, 8), 8), :]
            high = jnp.floor(code * (1.0 / LOW))
            at = pl.ds(pl.multiple_of(q * local + i * 8, 8), 8)
            hi_ref[at, base:base + count_rows] = high
            lo_ref[at, base:base + count_rows] = code - LOW * high
            return 0

        lax.fori_loop(0, local // 8, body, 0)

    weights(meta_ref, 0)
    for q in range(chips):
        split(ct_ref, pl.multiple_of((2 * q + core) * local, local), q, 0)
    swaps[0].wait_recv()
    weights(meta_in, count_rows)
    for q in range(chips):
        swaps[1 + q].wait_recv()
        split(ct_in, q * local, q, count_rows)

    hi_of = lax.div(lax.broadcasted_iota(jnp.int32, (HIGH * TN, CHUNK), 0), TN).astype(jnp.float32).astype(jnp.bfloat16)
    lo_of = lax.broadcasted_iota(jnp.int32, (LOW, CHUNK), 0).astype(jnp.float32).astype(jnp.bfloat16)
    one = jnp.ones((), jnp.bfloat16)
    zero = jnp.zeros((), jnp.bfloat16)
    first_half = lax.broadcasted_iota(jnp.int32, (HIGH * TN, 2 * LOW), 1) < LOW

    def compute(out, owner, offset, adds):
        first = owner * local + offset

        def body(g, _):
            f0 = first + g * GROUP
            low_sum = [None] * (GROUP // 2)
            high_sum = [None] * (GROUP // 2)
            for c in range(2 * count_rows // CHUNK):
                at = slice(c * CHUNK, (c + 1) * CHUNK)
                w = w_ref[:, at]
                a, b = [], []
                for k in range(GROUP):
                    high = jnp.broadcast_to(hi_ref[pl.ds(f0 + k, 1), at], (HIGH * TN, CHUNK)).astype(jnp.bfloat16)
                    low = jnp.broadcast_to(lo_ref[pl.ds(f0 + k, 1), at], (LOW, CHUNK)).astype(jnp.bfloat16)
                    a.append(jnp.where(high == hi_of, w, zero))
                    b.append(jnp.where(low == lo_of, one, zero))
                r = lax.dot_general(jnp.concatenate(a, axis=0), jnp.concatenate(b, axis=0),
                                    (((1,), (1,)), ((), ())), preferred_element_type=jnp.float32)
                size = HIGH * TN
                for p in range(GROUP // 2):
                    cols = slice(2 * LOW * p, 2 * LOW * (p + 1))
                    v = jnp.where(first_half, r[2 * p * size:(2 * p + 1) * size, cols],
                                  r[(2 * p + 1) * size:(2 * p + 2) * size, cols])
                    top = jnp.floor(v * (1.0 / PACK))
                    rest = v - PACK * top
                    low_sum[p] = rest if c == 0 else low_sum[p] + rest
                    high_sum[p] = top if c == 0 else high_sum[p] + top
            for p in range(GROUP // 2):
                slot = g * (GROUP // 2) + p
                value = jnp.concatenate([low_sum[p], high_sum[p]], axis=0)
                for add in adds:
                    value = value + add[slot]
                out[slot] = value
            return 0

        lax.fori_loop(0, half // GROUP, body, 0)

    n1a = (xs - 1) * ys
    n1b = (ys - 1) * xs
    slots = n1a + n1b + (ys - 1) + (xs - 1)

    def xy_round(rd):
        base = rd * slots
        offa = rd * 2 * half
        offb = offa + half
        copies = {}

        def go(slot, device):
            s = base + slot
            copies[slot] = send(sbuf.at[s], rbuf.at[s], xy_s.at[s], xy_r.at[s], device)

        def a_slot(dx, dy):
            return (dx - 1) * ys + dy

        def b_slot(dy, dx):
            return n1a + (dy - 1) * xs + dx

        def c_slot(dy):
            return n1a + n1b + dy - 1

        def d_slot(dx):
            return n1a + n1b + ys - 1 + dx - 1

        units = []

        def unit_a(dx, dy):
            xx, yy = lax.rem(x + dx, xs), lax.rem(y + dy, ys)
            s = a_slot(dx, dy)
            compute(sbuf.at[base + s], yy * xs + xx, offa, [])
            go(s, dev(y, xx))

        def unit_b(dy, dx):
            xx, yy = lax.rem(x + dx, xs), lax.rem(y + dy, ys)
            s = b_slot(dy, dx)
            compute(sbuf.at[base + s], yy * xs + xx, offb, [])
            go(s, dev(yy, x))

        def landed(s):
            copies[s].wait_recv()
            return rbuf.at[base + s]

        def unit_c(dy):
            yy = lax.rem(y + dy, ys)
            s = c_slot(dy)
            adds = [landed(a_slot(dx, dy)) for dx in range(1, xs)]
            compute(sbuf.at[base + s], yy * xs + x, offa, adds)
            go(s, dev(yy, x))

        def unit_d(dx):
            xx = lax.rem(x + dx, xs)
            s = d_slot(dx)
            adds = [landed(b_slot(dy, dx)) for dy in range(1, ys)]
            compute(sbuf.at[base + s], y * xs + xx, offb, adds)
            go(s, dev(y, xx))

        def own(which):
            if which == 0:
                near = [landed(a_slot(dx, 0)) for dx in range(1, xs)]
            else:
                near = [landed(b_slot(dy, 0)) for dy in range(1, ys)]
            compute(zbuf.at[rd, pl.ds(which * pairs, pairs)], chip, offb if which else offa, near)

        def own_late(which):
            far = [landed(c_slot(dy)) for dy in range(1, ys)] if which == 0 else [landed(d_slot(dx)) for dx in range(1, xs)]

            def body(i, _):
                value = zbuf[rd, which * pairs + i]
                for ref in far:
                    value = value + ref[i]
                zbuf[rd, which * pairs + i] = value
                return 0

            lax.fori_loop(0, pairs, body, 0)

        stage_a = [functools.partial(unit_a, dx, dy) for dy in range(ys - 1, -1, -1) for dx in range(1, xs)]
        stage_b = [functools.partial(unit_b, dy, dx) for dx in range(xs - 1, -1, -1) for dy in range(1, ys)]
        for i in range(max(len(stage_a), len(stage_b))):
            units += stage_a[i:i + 1] + stage_b[i:i + 1]
        stage_c = [functools.partial(unit_c, dy) for dy in range(1, ys)]
        stage_d = [functools.partial(unit_d, dx) for dx in range(1, xs)]
        for i in range(max(len(stage_c), len(stage_d))):
            units += stage_c[i:i + 1] + stage_d[i:i + 1]
        units += [functools.partial(own, 0), functools.partial(own, 1)]
        lates = [functools.partial(own_late, 0), functools.partial(own_late, 1)]
        return units, lates

    def add_block(rd, j, ref):
        def body(i, _):
            zbuf[rd, j * zb + i] = zbuf[rd, j * zb + i] + ref[rd, j, i]
            return 0

        lax.fori_loop(0, zb, body, 0)

    def up_copy(rd, j):
        return pltpu.make_async_remote_copy(
            src_ref=zbuf.at[rd, pl.ds(j * zb, zb)], dst_ref=zup.at[rd, j],
            send_sem=up_s.at[rd * rows + j], recv_sem=up_r.at[rd * rows + j],
            device_id=row_peer(1), device_id_type=MESH)

    def down_copy(rd, j):
        return pltpu.make_async_remote_copy(
            src_ref=zbuf.at[rd, pl.ds(j * zb, zb)], dst_ref=zdown.at[rd, j],
            send_sem=down_s.at[rd * rows + j], recv_sem=down_r.at[rd * rows + j],
            device_id=row_peer(rows - 1), device_id_type=MESH)

    def z_part(rd, i):
        j = rows - 1 - i

        @pl.when(z <= j)
        def _():
            @pl.when(z > 0)
            def _():
                up_copy(rd, j).wait_recv()
                add_block(rd, j, zup)

            @pl.when(z < j)
            def _():
                up_copy(rd, j).start()

        @pl.when(z >= i)
        def _():
            @pl.when(z < rows - 1)
            def _():
                down_copy(rd, i).wait_recv()
                add_block(rd, i, zdown)

            @pl.when(z > i)
            def _():
                down_copy(rd, i).start()

    def z_sent(rd):
        for j in range(rows):
            @pl.when(z < j)
            def _():
                up_copy(rd, j).wait_send()

            @pl.when(z > j)
            def _():
                down_copy(rd, j).wait_send()

    lane_r = lax.broadcasted_iota(jnp.int32, (2 * LOW, 2 * LOW), 0)
    lane_c = lax.broadcasted_iota(jnp.int32, (2 * LOW, 2 * LOW), 1)
    same = lax.div(lane_r, LOW) == lax.div(lane_c, LOW)
    upper = jnp.where(same & (lane_r <= lane_c), 1.0, 0.0)
    whole = jnp.where(same, 1.0, 0.0)
    left_lanes = lax.broadcasted_iota(jnp.int32, (TN, 2 * LOW), 1) < LOW

    def gains(rd):
        def body(i, _):
            h = zbuf[rd, z * zb + i]
            inner = jnp.dot(h, upper, precision=lax.Precision.HIGHEST, preferred_element_type=jnp.float32)
            sums = jnp.dot(h, whole, precision=lax.Precision.HIGHEST, preferred_element_type=jnp.float32)
            left = [[None] * HIGH for _ in range(CLASSES)]
            total = []
            for c in range(CLASSES):
                carry = jnp.zeros((TN, 2 * LOW), jnp.float32)
                for k in range(HIGH):
                    at = (c * HIGH + k) * TN
                    left[c][k] = inner[at:at + TN] + carry
                    carry = carry + sums[at:at + TN]
                total.append(carry)
            n_total = total[0] + total[1]
            safe = jnp.maximum(n_total, 1.0)
            best = None
            for k in range(HIGH):
                n_left = left[0][k] + left[1][k]
                n_right = n_total - n_left
                frac = n_left / safe
                scaled = n_total / (jnp.maximum(n_left, 1.0) * jnp.maximum(n_right, 1.0))
                spread = (left[0][k] - total[0] * frac) ** 2 * scaled + (left[1][k] - total[1] * frac) ** 2 * scaled
                best = spread if best is None else jnp.maximum(best, spread)
            even = jnp.max(jnp.where(left_lanes, best, 0.0), axis=1, keepdims=True)
            odd = jnp.max(jnp.where(left_lanes, 0.0, best), axis=1, keepdims=True)
            gbuf[0, rd * zb + i] = jnp.where(left_lanes, even, odd)
            return 0

        lax.fori_loop(0, zb, body, 0)

    previous = None
    for rd in range(rounds):
        units, lates = xy_round(rd)
        parts = [] if previous is None else [functools.partial(z_part, previous, i) for i in range(rows)]
        every = max(1, len(units) // (len(parts) + 1))
        for n, unit in enumerate(units):
            unit()
            if parts and (n + 1) % every == 0:
                parts.pop(0)()
        for part in parts:
            part()
        if previous is not None:
            gains(previous)
        for late in lates:
            late()
        previous = rd
    for i in range(rows):
        z_part(previous, i)
    gains(previous)

    size = rounds * zb
    copies = [send(gbuf.at[0], gbuf.at[k], g_s.at[k], g_r.at[k], row_peer(k)) for k in range(1, rows)]
    for copy in copies:
        copy.wait_recv()
    top = None
    for k in range(rows):
        origin = lax.rem(z - k + rows, rows)
        for rd in range(rounds):
            for i in range(zb):
                value = gbuf[k, rd * zb + i]
                fg_ref[rd * rows * zb + origin * zb + i] = value
                top = value if top is None else jnp.maximum(top, value)
    mbuf[...] = jnp.broadcast_to(jnp.max(top, axis=1, keepdims=True), (TN, 2 * LOW))
    copies = [send(mbuf, min_ref.at[k], m_s.at[k], m_r.at[k], feat_peer(k)) for k in range(1, feat)]
    best = mbuf[...]
    for k in range(1, feat):
        copies[k - 1].wait_recv()
        best = jnp.maximum(best, min_ref[k])
    node_ref[...] = best
    for copy in pending:
        copy.wait_send()
    for rd in range(rounds):
        z_sent(rd)


def on_device(rows, feat, codes, node_ids, bag_counts, labels):
    count_rows, features = codes.shape
    chips, xs, ys, local, rounds = plan(rows, feat, features)
    half = local // rounds // 2
    pairs = half // 2
    zb = half * 2 // rows // 2
    slots = (xs - 1) * ys + (ys - 1) * xs + (ys - 1) + (xs - 1)
    tile = (CLASSES * HIGH * TN, 2 * LOW)
    ct = jnp.transpose(codes).astype(jnp.float32)
    meta = jnp.concatenate([node_ids, bag_counts, labels[None], jnp.zeros((3, count_rows), jnp.int32)], axis=0).astype(jnp.float32)
    vmem = pl.BlockSpec(memory_space=pltpu.VMEM)
    dma = lambda n: pltpu.SemaphoreType.DMA((n,))
    f32 = jnp.float32
    fg, node = pl.pallas_call(
        functools.partial(kernel, rows, feat, features, count_rows),
        out_shape=(jax.ShapeDtypeStruct((local // 2, TN, 2 * LOW), f32), jax.ShapeDtypeStruct((TN, 2 * LOW), f32)),
        in_specs=[vmem, vmem],
        out_specs=(vmem, vmem),
        scratch_shapes=[
            pltpu.VMEM((features // 2, count_rows), f32),
            pltpu.VMEM(meta.shape, f32),
            pltpu.VMEM((features // 2, 2 * count_rows), f32),
            pltpu.VMEM((features // 2, 2 * count_rows), f32),
            pltpu.VMEM((HIGH * TN, 2 * count_rows), jnp.bfloat16),
            pltpu.VMEM((rounds * slots, pairs) + tile, f32),
            pltpu.VMEM((rounds * slots, pairs) + tile, f32),
            pltpu.VMEM((rounds, 2 * pairs) + tile, f32),
            pltpu.VMEM((rounds, rows, zb) + tile, f32),
            pltpu.VMEM((rounds, rows, zb) + tile, f32),
            pltpu.VMEM((rows, rounds * zb, TN, 2 * LOW), f32),
            pltpu.VMEM((TN, 2 * LOW), f32),
            pltpu.VMEM((feat, TN, 2 * LOW), f32),
            dma(chips + 1), dma(chips + 1),
            dma(rounds * slots), dma(rounds * slots),
            dma(rounds * rows), dma(rounds * rows), dma(rounds * rows), dma(rounds * rows),
            dma(rows), dma(rows), dma(feat), dma(feat),
        ],
        compiler_params=pltpu.CompilerParams(
            collective_id=0, has_side_effects=True, vmem_limit_bytes=60 * 1024 * 1024),
    )(ct, meta)
    both = jnp.stack([fg[:, :, 0], fg[:, :, LOW]], axis=1)
    feature_gain = jnp.transpose(both.reshape(local, TN)).reshape(TREES, NODES, local)
    return feature_gain, node[:, 0].reshape(TREES, NODES)


def solution(mesh):
    return jax.shard_map(
        functools.partial(on_device, mesh.shape["rows"], mesh.shape["feat"]),
        mesh=mesh,
        in_specs=(
            P(("rows", "feat"), None),
            P(None, ("rows", "feat")),
            P(None, ("rows", "feat")),
            P(("rows", "feat")),
        ),
        out_specs=(P(None, None, "feat"), P()),
        check_vma=False,
    )
```

time: 461 us -> 164 us (0.36)
  matrix products: 271 us -> 0 us
  Pallas kernels: 0 us -> 148 us
  waiting for transfers between devices: 129 us -> 0 us
  local copies, waits for them, and re-layouts: 25.5 us -> 8.97 us
  blocking collectives: 14.3 us -> 0 us
  between operations: 14.2 us -> 0.67 us
    dot_general x17 -> x0, matrix products: 271 us -> none  [the longest x16 269 us: one_block(): jnp.einsum('rfb,rs->fsb', onehot, weights, preferred_element_type=jnp.flo...]
    pallas_call x0 -> x1, Pallas kernels: none -> 148 us  [on_device(): pl.pallas_call(functools.partial(kernel, rows, feat, features, count_rows...]
    reduce_scatter x1 -> x0, waiting for transfers between devices: 74.3 us -> none  [on_device(): lax.psum_scatter(histogram_of(codes, weights), 'feat', scatter_dimension=...]
    psum x1 -> x0, waiting for transfers between devices: 54.3 us -> none  [on_device(): hist = lax.psum(partial_hist, 'rows')]
    eq x16 -> x0, local copies, waits for them, and re-layouts: 15.5 us -> none  [one_block(): onehot = (column_block[:, :, None] == bin_index).astype(jnp.bfloat16)]
    pmax x1 -> x0, blocking collectives: 14.3 us -> none  [on_device(): node_gain = lax.pmax(jnp.max(feature_gain, axis=2), 'feat')]
    convert_element_type x17 -> x2, other arithmetic: 0.83 us -> 6.1 us  [the longest x1 4.66 us: on_device(): ct = jnp.transpose(codes).astype(jnp.float32)]
  transfers between devices with their start and end apart: 2 -> 0, of which waited for: 2 -> 0; matrix products, arithmetic and copies ran while one was open for 0% -> 0% of each run, Pallas kernels for 0% -> 0%
where the time goes in v1:
time: 164 us; the launch traced here: 163 us
  Pallas kernels  148 us (90%)
  local copies, waits for them, and re-layouts  8.97 us (5%)
  other arithmetic  6.11 us (4%)
    pallas_call x1, Pallas kernels, on_device(): pl.pallas_call(functools.partial(kernel, rows, feat, features, count_rows...  148 us
    unnamed x1, local copies, waits for them, and re-layouts  5.37 us
    convert_element_type x1, other arithmetic, on_device(): ct = jnp.transpose(codes).astype(jnp.float32)  4.66 us

profile of v1, /device:TPU:0, one launch (start us, length us, event | category | flops | bytes accessed | tf_op | source)
XLA Modules:
  0.0 163.4 jit_solution(6711809312409416670)
XLA Ops:
  0.6 0.1 pad.5.clone
  0.7 1.4 add_convert_fusion.meta_ref
  2.2 5.4 %copy.13 = s32[2048,512]{0,1:T(8,128)} copy(s32[2048,512]{1,0:T(8,128)} %param.4) | data formatting | bytes 8388608 | tf_op args[0]
  7.5 4.7 %convert_bitcast_fusion.ct_ref = f32[512,2048]{1,0:T(8,128)} fusion(s32[2048,512]{0,1:T(8,128)} %copy.13), kind=kLoop, calls=%fused_computation | loop fusion | flops 1048576 | bytes 8388608 | tf_op jit(solution)/shard_map/convert_element_type | solution.py:393
  12.2 147.6 %shard_map.59 = (f32[32,8,128]{2,1,0:T(8,128)}, f32[8,128]{1,0:T(8,128)}) custom-call(f32[512,2048]{1,0:T(8,128)} %convert_bitcast_fusion.ct_ref, f32[8,2048]{1,0:T(8,128)} %add_convert_fusion.meta_ref), custom_call_target="tpu_custom_call" | custom-call | tf_op jit(solution)/shard_map/pallas_call | solution.py:398
  159.8 0.8 slice_reduce_fusion
  160.6 0.6 reshape_squeeze.3
  161.3 1.1 fusion
  162.3 0.1 copy.14
  162.5 0.1 copy.15
  162.6 0.1 copy.16
  162.7 0.7 copy.17
  (2 shorter events, 0.0 us)

commit v2 on v1

--- a/solution.py
+++ b/solution.py
@@ -31,8 +31,8 @@
 
 
 def kernel(rows, feat, features, count_rows, ct_ref, meta_ref, fg_ref, node_ref,
-           ct_in, meta_in, hi_ref, lo_ref, w_ref, sbuf, rbuf, zbuf, zup, zdown, gbuf, mbuf, min_ref,
-           core_s, core_r, xy_s, xy_r, up_s, up_r, down_s, down_r, g_s, g_r, m_s, m_r):
+           ct_in, meta_in, hi_ref, lo_ref, w_ref, sbuf, rbuf, zbuf, zin, gbuf, mbuf, min_ref,
+           core_s, core_r, xy_s, xy_r, z_s, z_r, g_s, g_r, m_s, m_r):
     chips, xs, ys, local, rounds = plan(rows, feat, features)
     half = local // rounds // 2
     pairs = half // 2
@@ -96,10 +96,10 @@
     def split(src, start, q, base):
         def body(i, _):
             code = src[pl.ds(pl.multiple_of(start + i * 8, 8), 8), :]
-            high = jnp.floor(code * (1.0 / LOW))
+            high = lax.shift_right_logical(code, LOW.bit_length() - 1)
             at = pl.ds(pl.multiple_of(q * local + i * 8, 8), 8)
-            hi_ref[at, base:base + count_rows] = high
-            lo_ref[at, base:base + count_rows] = code - LOW * high
+            hi_ref[at, base:base + count_rows] = high.astype(jnp.float32)
+            lo_ref[at, base:base + count_rows] = (code & (LOW - 1)).astype(jnp.float32)
             return 0
 
         lax.fori_loop(0, local // 8, body, 0)
@@ -135,7 +135,8 @@
                     low = jnp.broadcast_to(lo_ref[pl.ds(f0 + k, 1), at], (LOW, CHUNK)).astype(jnp.bfloat16)
                     a.append(jnp.where(high == hi_of, w, zero))
                     b.append(jnp.where(low == lo_of, one, zero))
-                r = lax.dot_general(jnp.concatenate(a, axis=0), jnp.concatenate(b, axis=0),
+                ones = jnp.concatenate(b, axis=0).astype(jnp.float8_e4m3fn)
+                r = lax.dot_general(jnp.concatenate(a, axis=0), ones,
                                     (((1,), (1,)), ((), ())), preferred_element_type=jnp.float32)
                 size = HIGH * TN
                 for p in range(GROUP // 2):
@@ -245,60 +246,17 @@
         lates = [functools.partial(own_late, 0), functools.partial(own_late, 1)]
         return units, lates
 
-    def add_block(rd, j, ref):
-        def body(i, _):
-            zbuf[rd, j * zb + i] = zbuf[rd, j * zb + i] + ref[rd, j, i]
-            return 0
-
-        lax.fori_loop(0, zb, body, 0)
-
-    def up_copy(rd, j):
-        return pltpu.make_async_remote_copy(
-            src_ref=zbuf.at[rd, pl.ds(j * zb, zb)], dst_ref=zup.at[rd, j],
-            send_sem=up_s.at[rd * rows + j], recv_sem=up_r.at[rd * rows + j],
-            device_id=row_peer(1), device_id_type=MESH)
-
-    def down_copy(rd, j):
-        return pltpu.make_async_remote_copy(
-            src_ref=zbuf.at[rd, pl.ds(j * zb, zb)], dst_ref=zdown.at[rd, j],
-            send_sem=down_s.at[rd * rows + j], recv_sem=down_r.at[rd * rows + j],
-            device_id=row_peer(rows - 1), device_id_type=MESH)
-
-    def z_part(rd, i):
-        j = rows - 1 - i
-
-        @pl.when(z <= j)
-        def _():
-            @pl.when(z > 0)
-            def _():
-                up_copy(rd, j).wait_recv()
-                add_block(rd, j, zup)
-
-            @pl.when(z < j)
-            def _():
-                up_copy(rd, j).start()
-
-        @pl.when(z >= i)
-        def _():
-            @pl.when(z < rows - 1)
-            def _():
-                down_copy(rd, i).wait_recv()
-                add_block(rd, i, zdown)
-
-            @pl.when(z > i)
-            def _():
-                down_copy(rd, i).start()
-
-    def z_sent(rd):
-        for j in range(rows):
-            @pl.when(z < j)
-            def _():
-                up_copy(rd, j).wait_send()
-
-            @pl.when(z > j)
-            def _():
-                down_copy(rd, j).wait_send()
-
+    def z_start(rd):
+        for k in range(1, rows):
+            j = lax.rem(z + k, rows)
+            n = rd * rows + k
+            zcopies[n] = send(zbuf.at[rd, pl.ds(j * zb, zb)], zin.at[rd, k], z_s.at[n], z_r.at[n], row_peer(k))
+
+    def z_landed(rd):
+        for k in range(1, rows):
+            zcopies[rd * rows + k].wait_recv()
+
+    zcopies = {}
     lane_r = lax.broadcasted_iota(jnp.int32, (2 * LOW, 2 * LOW), 0)
     lane_c = lax.broadcasted_iota(jnp.int32, (2 * LOW, 2 * LOW), 1)
     same = lax.div(lane_r, LOW) == lax.div(lane_c, LOW)
@@ -307,10 +265,16 @@
     left_lanes = lax.broadcasted_iota(jnp.int32, (TN, 2 * LOW), 1) < LOW
 
     def gains(rd):
-        def body(i, _):
-            h = zbuf[rd, z * zb + i]
-            inner = jnp.dot(h, upper, precision=lax.Precision.HIGHEST, preferred_element_type=jnp.float32)
-            sums = jnp.dot(h, whole, precision=lax.Precision.HIGHEST, preferred_element_type=jnp.float32)
+        block = CLASSES * HIGH * TN
+        h = zbuf[rd, pl.ds(z * zb, zb)]
+        for k in range(1, rows):
+            h = h + zin[rd, k]
+        h = h.reshape(zb * block, 2 * LOW)
+        inner_all = jnp.dot(h, upper, precision=lax.Precision.HIGHEST, preferred_element_type=jnp.float32)
+        sums_all = jnp.dot(h, whole, precision=lax.Precision.HIGHEST, preferred_element_type=jnp.float32)
+        for i in range(zb):
+            inner = inner_all[i * block:(i + 1) * block]
+            sums = sums_all[i * block:(i + 1) * block]
             left = [[None] * HIGH for _ in range(CLASSES)]
             total = []
             for c in range(CLASSES):
@@ -333,31 +297,22 @@
             even = jnp.max(jnp.where(left_lanes, best, 0.0), axis=1, keepdims=True)
             odd = jnp.max(jnp.where(left_lanes, 0.0, best), axis=1, keepdims=True)
             gbuf[0, rd * zb + i] = jnp.where(left_lanes, even, odd)
-            return 0
-
-        lax.fori_loop(0, zb, body, 0)
 
     previous = None
     for rd in range(rounds):
         units, lates = xy_round(rd)
-        parts = [] if previous is None else [functools.partial(z_part, previous, i) for i in range(rows)]
-        every = max(1, len(units) // (len(parts) + 1))
-        for n, unit in enumerate(units):
+        for unit in units:
             unit()
-            if parts and (n + 1) % every == 0:
-                parts.pop(0)()
-        for part in parts:
-            part()
-        if previous is not None:
-            gains(previous)
         for late in lates:
             late()
+        z_start(rd)
+        if previous is not None:
+            z_landed(previous)
+            gains(previous)
         previous = rd
-    for i in range(rows):
-        z_part(previous, i)
+    z_landed(previous)
     gains(previous)
 
-    size = rounds * zb
     copies = [send(gbuf.at[0], gbuf.at[k], g_s.at[k], g_r.at[k], row_peer(k)) for k in range(1, rows)]
     for copy in copies:
         copy.wait_recv()
@@ -378,8 +333,6 @@
     node_ref[...] = best
     for copy in pending:
         copy.wait_send()
-    for rd in range(rounds):
-        z_sent(rd)
 
 
 def on_device(rows, feat, codes, node_ids, bag_counts, labels):
@@ -390,7 +343,7 @@
     zb = half * 2 // rows // 2
     slots = (xs - 1) * ys + (ys - 1) * xs + (ys - 1) + (xs - 1)
     tile = (CLASSES * HIGH * TN, 2 * LOW)
-    ct = jnp.transpose(codes).astype(jnp.float32)
+    ct = jnp.transpose(codes)
     meta = jnp.concatenate([node_ids, bag_counts, labels[None], jnp.zeros((3, count_rows), jnp.int32)], axis=0).astype(jnp.float32)
     vmem = pl.BlockSpec(memory_space=pltpu.VMEM)
     dma = lambda n: pltpu.SemaphoreType.DMA((n,))
@@ -401,7 +354,7 @@
         in_specs=[vmem, vmem],
         out_specs=(vmem, vmem),
         scratch_shapes=[
-            pltpu.VMEM((features // 2, count_rows), f32),
+            pltpu.VMEM((features // 2, count_rows), jnp.int32),
             pltpu.VMEM(meta.shape, f32),
             pltpu.VMEM((features // 2, 2 * count_rows), f32),
             pltpu.VMEM((features // 2, 2 * count_rows), f32),
@@ -410,13 +363,12 @@
             pltpu.VMEM((rounds * slots, pairs) + tile, f32),
             pltpu.VMEM((rounds, 2 * pairs) + tile, f32),
             pltpu.VMEM((rounds, rows, zb) + tile, f32),
-            pltpu.VMEM((rounds, rows, zb) + tile, f32),
             pltpu.VMEM((rows, rounds * zb, TN, 2 * LOW), f32),
             pltpu.VMEM((TN, 2 * LOW), f32),
             pltpu.VMEM((feat, TN, 2 * LOW), f32),
             dma(chips + 1), dma(chips + 1),
             dma(rounds * slots), dma(rounds * slots),
-            dma(rounds * rows), dma(rounds * rows), dma(rounds * rows), dma(rounds * rows),
+            dma(rounds * rows), dma(rounds * rows),
             dma(rows), dma(rows), dma(feat), dma(feat),
         ],
         compiler_params=pltpu.CompilerParams(

time: 164 us -> 90.8 us (0.55)
  Pallas kernels: 148 us -> 79.4 us
  other arithmetic: 6.11 us -> 1.45 us
    pallas_call x1, Pallas kernels: 148 us -> 79.4 us  [on_device(): pl.pallas_call(functools.partial(kernel, rows, feat, features, count_rows...]
    convert_element_type x1 -> x0, other arithmetic: 4.66 us -> none  [on_device(): ct = jnp.transpose(codes).astype(jnp.float32)]
where the time goes in v2:
time: 90.8 us; the launch traced here: 90.4 us
  Pallas kernels  79.4 us (87%)
  local copies, waits for them, and re-layouts  8.97 us (10%)
  other arithmetic  1.45 us (2%)
    pallas_call x1, Pallas kernels, on_device(): pl.pallas_call(functools.partial(kernel, rows, feat, features, count_rows...  79.4 us
    unnamed x1, local copies, waits for them, and re-layouts  5.37 us

profile of v2, /device:TPU:0, one launch (start us, length us, event | category | flops | bytes accessed | tf_op | source)
XLA Modules:
  0.0 90.4 jit_solution(11025101820999562978)
XLA Ops:
  0.6 0.1 pad.5.clone
  0.7 1.4 %add_convert_fusion.meta_ref = f32[8,2048]{1,0:T(8,128)} fusion(s32[1,2048]{1,0:T(1,128)} %bitcast.12, s32[2,2048]{1,0:T(2,128)} %param.6, s32[2,2048]{1,0:T(2,128)} %param.5, s32[8]{0:T(128)S(1)} %pad.5.clone), kind=kLoop, calls=%fused_computation | loop fusion | flops 65536 | bytes 106528 | tf_op jit(solution)/shard_map/convert_element_type | solution.py:347
  2.2 5.4 %copy.13 = s32[2048,512]{0,1:T(8,128)} copy(s32[2048,512]{1,0:T(8,128)} %param.4) | data formatting | bytes 8388608 | tf_op args[0]
  7.5 79.4 %shard_map.59 = (f32[32,8,128]{2,1,0:T(8,128)}, f32[8,128]{1,0:T(8,128)}) custom-call(s32[512,2048]{1,0:T(8,128)} %bitcast.8, f32[8,2048]{1,0:T(8,128)} %add_convert_fusion.meta_ref), custom_call_target="tpu_custom_call" | custom-call | tf_op jit(solution)/shard_map/pallas_call | solution.py:351
  86.9 0.8 slice_reduce_fusion
  87.7 0.6 reshape_squeeze.3
  88.3 1.1 %fusion = (f32[32,8,1]{2,1,0:T(8,128)S(1)}, f32[32,8,1]{2,1,0:T(8,128)S(1)}) fusion(f32[32,8,128]{2,1,0:T(8,128)} %get-tuple-element.4), kind=kLoop, calls=%fused_computation.3 | loop fusion | bytes 4096 | tf_op jit(solution)/shard_map/slice | solution.py:377
  89.4 0.1 copy.14
  89.5 0.1 copy.15
  89.7 0.1 copy.16
  89.8 0.7 copy.17
  (2 shorter events, 0.0 us)
